TPU v7x, 32 devices: a whole 2x2x4 slice. The times are simulated.
32 devices in a mesh: px: 8 (over z, x), py: 4 (over y, core).
Axes of the slice: x: 2, y: 2, z: 4, core: 2. Of those that a mesh axis runs over, the one named last changes fastest.
Arguments:
- potential: float32 [256, 256, 256], P(('px', 'py')), may hold values from 0 to 1
- recovery: float32 [256, 256, 256], P(('px', 'py')), may hold values from 0 to 2
- stimulus: float32 [256, 256, 256], P(('px', 'py')), may hold values from -8 to 8
- conductivity: float32 [256, 256, 256], P('px', 'py'), may hold values from 0.2 to 5
Outputs:
- potential_next: float32 [256, 256, 256], P(('px', 'py'))
- recovery_next: float32 [256, 256, 256], P(('px', 'py'))
All inputs are finite; a program needn't handle non-finite values.
Results may differ from a plain program's by a relative error of at most 0.0003.
Values sent between devices are 32-bit elements; how exact they have to be, the bound alone decides.
A program may use at most 128 MiB of HBM per device.

v0:
```python
import math

import jax
import jax.numpy as jnp
from jax import lax
from jax.sharding import PartitionSpec as P

GX = 256
GY = 256
GZ = 256
ITERS = 4


mass_rate = 0.01
mean_conduct = 1.0
excite_gain = 8.0
threshold = 0.15
base_rate = 0.002
rate_slope = 0.2
rate_shift = 0.3
time_step = 0.1
forms = ("xyz,xk->kyz", "xyz,yk->xkz", "xyz,zk->xyk")


def padded_2(cells, sides, width):
    for axis, dim in sides:
        count = lax.axis_size(axis)
        head = lax.slice_in_dim(cells, 0, width, axis=dim)
        tail = lax.slice_in_dim(cells, cells.shape[dim] - width, cells.shape[dim], axis=dim)
        cells = jnp.concatenate(
            [
                lax.ppermute(tail, axis, [(i, (i + 1) % count) for i in range(count)]),
                cells,
                lax.ppermute(head, axis, [((i + 1) % count, i) for i in range(count)]),
            ],
            axis=dim,
        )
    return cells


def dft_tables(length):
    steps = jnp.arange(length, dtype=jnp.int32)
    phase = steps[:, None] * steps[None, :] % length
    angle = 2.0 * math.pi / length * phase.astype(jnp.float32)
    return (jnp.cos(angle), jnp.sin(angle))


def cas_table(length):
    cosine, sine = dft_tables(length)
    return cosine + sine


def along(field, table, dimension):
    return jnp.einsum(forms[dimension], field, table, precision=lax.Precision.HIGHEST)


def wave_term(length, start, count):
    modes = start + jnp.arange(count, dtype=jnp.int32)
    return 2.0 - 2.0 * jnp.cos(2.0 * math.pi / length * modes.astype(jnp.float32))


def precondition_cas(residual, x_cas, y_cas, z_cas):
    spectrum = along(residual, z_cas, 2)
    spectrum = along(
        lax.all_to_all(spectrum, "py", split_axis=2, concat_axis=1, tiled=True), y_cas, 1
    )
    spectrum = along(
        lax.all_to_all(spectrum, "px", split_axis=1, concat_axis=0, tiled=True), x_cas, 0
    )
    count_y = spectrum.shape[1]
    count_z = spectrum.shape[2]
    symbol = mass_rate + mean_conduct * (
        wave_term(GX, 0, GX)[:, None, None]
        + wave_term(GY, lax.axis_index("px") * count_y, count_y)[None, :, None]
        + wave_term(GZ, lax.axis_index("py") * count_z, count_z)[None, None, :]
    )
    spectrum = along(spectrum / symbol, x_cas, 0) * (1.0 / GX)
    spectrum = along(
        lax.all_to_all(spectrum, "px", split_axis=0, concat_axis=1, tiled=True), y_cas, 1
    ) * (1.0 / GY)
    return along(
        lax.all_to_all(spectrum, "py", split_axis=1, concat_axis=2, tiled=True), z_cas, 2
    ) * (1.0 / GZ)


def local(potential, recovery, stimulus, conductivity):
    drive = (
        excite_gain * potential * (potential - threshold) * (1.0 - potential) - potential * recovery
    )
    v_star = potential + time_step * (drive + stimulus)
    rate = base_rate + rate_slope * recovery / (potential + rate_shift)
    recovery_next = recovery + time_step * rate * (
        -recovery - excite_gain * potential * (potential - threshold - 1.0)
    )
    start_field = lax.all_to_all(v_star, "py", split_axis=1, concat_axis=0, tiled=True)
    cond_pad = padded_2(conductivity, (("px", 0), ("py", 1)), 1)
    face_xplus = 0.5 * (conductivity + cond_pad[2:, 1:-1])
    face_xminus = 0.5 * (conductivity + cond_pad[:-2, 1:-1])
    face_yplus = 0.5 * (conductivity + cond_pad[1:-1, 2:])
    face_yminus = 0.5 * (conductivity + cond_pad[1:-1, :-2])
    face_zplus = 0.5 * (conductivity + jnp.roll(conductivity, -1, 2))
    face_zminus = 0.5 * (conductivity + jnp.roll(conductivity, 1, 2))

    def operate(field):
        padded = padded_2(field, (("px", 0), ("py", 1)), 1)
        result_sum = mass_rate * field
        result_sum = (
            result_sum
            + face_xplus * (field - padded[2:, 1:-1])
            + face_xminus * (field - padded[:-2, 1:-1])
        )
        result_sum = (
            result_sum
            + face_yplus * (field - padded[1:-1, 2:])
            + face_yminus * (field - padded[1:-1, :-2])
        )
        result_sum = (
            result_sum
            + face_zplus * (field - jnp.roll(field, -1, 2))
            + face_zminus * (field - jnp.roll(field, 1, 2))
        )
        return result_sum

    x_cas = cas_table(GX)
    y_cas = cas_table(GY)
    z_cas = cas_table(GZ)

    def apply_inverse(residual):
        return precondition_cas(residual, x_cas, y_cas, z_cas)

    solution = start_field
    residual = mass_rate * start_field - operate(solution)

    def product_sum(residual, precond):
        return lax.psum(jnp.sum(residual * precond), ("px", "py"))

    precond = apply_inverse(residual)
    direction = precond
    product_now = product_sum(residual, precond)
    for step in range(ITERS):
        image = operate(direction)
        alpha = product_now / lax.psum(jnp.sum(direction * image), ("px", "py"))
        solution = solution + alpha * direction
        residual = residual - alpha * image
        if step < ITERS - 1:
            precond = apply_inverse(residual)
            product_next = product_sum(residual, precond)
            direction = precond + product_next / product_now * direction
            product_now = product_next
    potential_next = lax.all_to_all(solution, "py", split_axis=0, concat_axis=1, tiled=True)
    return (potential_next, recovery_next)


def solution(mesh):
    in_specs = (
        P(("px", "py"), None, None),
        P(("px", "py"), None, None),
        P(("px", "py"), None, None),
        P("px", "py", None),
    )
    out_specs = (P(("px", "py"), None, None), P(("px", "py"), None, None))
    return jax.shard_map(local, mesh=mesh, in_specs=in_specs, out_specs=out_specs, check_vma=False)
```

profile of v0, /device:TPU:0, one launch (start us, length us, event | category | flops | bytes accessed | tf_op | source)
XLA Modules:
  0.0 1881.2 jit_solution(16625585675331391221)
XLA Ops:
  0.6 9.3 multiply_add_fusion
  28.2 13.1 all-to-all-done
  55.5 14.4 fusion.63
  86.4 30.3 %all_to_all.324 = f32[4,1,131072]{2,1,0:T(1,128)} all-to-all(f32[4,1,131072]{2,1,0:T(1,128)} %reshape.95), channel_id=1, replica_groups=mesh['px'=8,'py'=4] {'py'}, dimensions={0} | all-to-all | bytes 4194304 | tf_op jit(solution)/shard_map/all_to_all | solution.py:65
  117.2 8.9 reduce
  155.5 7.2 reshape.97
  168.6 47.7 %all-to-all-done.2 = f32[8,1,65536]{2,1,0:T(1,128)} async-done(((f32[8,1,65536]{2,1,0:T(1,128)}), f32[8,1,65536]{2,1,0:T(1,128)}, u32[]{:S(2)}, u32[]{:S(2)}) %all-to-all-start.2) | async-done | bytes 2097184 | tf_op jit(solution)/shard_map/all_to_all | solution.py:68
  216.3 8.4 reduce.1
  256.3 7.2 reshape.99
  263.5 52.7 %all_to_all.325 = f32[8,1,65536]{2,1,0:T(1,128)} all-to-all(f32[8,1,65536]{2,1,0:T(1,128)} %reshape.99), channel_id=1, replica_groups=mesh['px'=8,'py'=4] {'px'}, dimensions={0} | all-to-all | bytes 4194304 | tf_op jit(solution)/shard_map/all_to_all | solution.py:79
  316.2 8.4 reduce.2
  355.6 30.1 %all_to_all.326 = f32[4,1,131072]{2,1,0:T(1,128)} all-to-all(f32[4,1,131072]{2,1,0:T(1,128)} %reshape.101), channel_id=1, replica_groups=mesh['px'=8,'py'=4] {'py'}, dimensions={0} | all-to-all | bytes 4194304 | tf_op jit(solution)/shard_map/all_to_all | solution.py:82
  385.7 8.9 reduce.3
  429.6 9.3 multiply_reduce_fusion.5
  438.9 38.9 %all-reduce = (f32[]{:T(128)}, f32[]{:T(128)}) all-reduce(f32[]{:T(128)} %get-tuple-element.5, f32[]{:T(128)} %get-tuple-element.4), channel_id=1, replica_groups=mesh['px'=8,'py'=4] {'px','py'}, use_global_device_ids=true, to_apply=%region_1.2 | all-reduce | flops 2 | bytes 16 | tf_op jit(solution)/shard_map/psum | solution.py:135
  498.2 30.3 %all_to_all.327 = f32[4,1,131072]{2,1,0:T(1,128)} all-to-all(f32[4,1,131072]{2,1,0:T(1,128)} %reshape.103), channel_id=1, replica_groups=mesh['px'=8,'py'=4] {'py'}, dimensions={0} | all-to-all | bytes 4194304 | tf_op jit(solution)/shard_map/all_to_all | solution.py:65
  528.5 8.9 reduce.4
  573.8 54.2 %all_to_all.328 = f32[8,1,65536]{2,1,0:T(1,128)} all-to-all(f32[8,1,65536]{2,1,0:T(1,128)} %reshape.105), channel_id=1, replica_groups=mesh['px'=8,'py'=4] {'px'}, dimensions={0} | all-to-all | bytes 4194304 | tf_op jit(solution)/shard_map/all_to_all | solution.py:68
  628.0 8.4 reduce.5
  675.5 52.0 %all_to_all.329 = f32[8,1,65536]{2,1,0:T(1,128)} all-to-all(f32[8,1,65536]{2,1,0:T(1,128)} %reshape.107), channel_id=1, replica_groups=mesh['px'=8,'py'=4] {'px'}, dimensions={0} | all-to-all | bytes 4194304 | tf_op jit(solution)/shard_map/all_to_all | solution.py:79
  727.4 8.4 reduce.6
  767.2 30.1 %all_to_all.330 = f32[4,1,131072]{2,1,0:T(1,128)} all-to-all(f32[4,1,131072]{2,1,0:T(1,128)} %reshape.109), channel_id=1, replica_groups=mesh['px'=8,'py'=4] {'py'}, dimensions={0} | all-to-all | bytes 4194304 | tf_op jit(solution)/shard_map/all_to_all | solution.py:82
  797.3 8.9 reduce.7
  831.1 38.9 %psum.58 = f32[]{:T(128)} all-reduce(f32[]{:T(128)} %get-tuple-element.70), channel_id=1, replica_groups=mesh['px'=8,'py'=4] {'px','py'}, use_global_device_ids=true, to_apply=%region_5.6 | all-reduce | flops 1 | bytes 8 | tf_op jit(solution)/shard_map/psum | solution.py:135
  891.9 40.2 %psum.59 = f32[]{:T(128)} all-reduce(f32[]{:T(128)} %get-tuple-element.10), channel_id=1, replica_groups=mesh['px'=8,'py'=4] {'px','py'}, use_global_device_ids=true, to_apply=%region_7.8 | all-reduce | flops 1 | bytes 8 | tf_op jit(solution)/shard_map/psum | solution.py:142
  952.5 30.3 %all_to_all.331 = f32[4,1,131072]{2,1,0:T(1,128)} all-to-all(f32[4,1,131072]{2,1,0:T(1,128)} %reshape.111), channel_id=1, replica_groups=mesh['px'=8,'py'=4] {'py'}, dimensions={0} | all-to-all | bytes 4194304 | tf_op jit(solution)/shard_map/all_to_all | solution.py:65
  982.9 8.9 reduce.8
  1021.2 7.2 reshape.113
  1028.3 54.2 %all_to_all.332 = f32[8,1,65536]{2,1,0:T(1,128)} all-to-all(f32[8,1,65536]{2,1,0:T(1,128)} %reshape.113), channel_id=1, replica_groups=mesh['px'=8,'py'=4] {'px'}, dimensions={0} | all-to-all | bytes 4194304 | tf_op jit(solution)/shard_map/all_to_all | solution.py:68
  1082.5 8.4 reduce.9
  1129.7 52.2 %all_to_all.333 = f32[8,1,65536]{2,1,0:T(1,128)} all-to-all(f32[8,1,65536]{2,1,0:T(1,128)} %reshape.115), channel_id=1, replica_groups=mesh['px'=8,'py'=4] {'px'}, dimensions={0} | all-to-all | bytes 4194304 | tf_op jit(solution)/shard_map/all_to_all | solution.py:79
  1181.9 8.4 reduce.10
  1221.5 30.1 %all_to_all.334 = f32[4,1,131072]{2,1,0:T(1,128)} all-to-all(f32[4,1,131072]{2,1,0:T(1,128)} %reshape.117), channel_id=1, replica_groups=mesh['px'=8,'py'=4] {'py'}, dimensions={0} | all-to-all | bytes 4194304 | tf_op jit(solution)/shard_map/all_to_all | solution.py:82
  1251.6 8.9 reduce.11
  1285.6 38.8 %psum.60 = f32[]{:T(128)} all-reduce(f32[]{:T(128)} %get-tuple-element.72), channel_id=1, replica_groups=mesh['px'=8,'py'=4] {'px','py'}, use_global_device_ids=true, to_apply=%region_9.10 | all-reduce | flops 1 | bytes 8 | tf_op jit(solution)/shard_map/psum | solution.py:135
  1346.5 40.3 %psum.61 = f32[]{:T(128)} all-reduce(f32[]{:T(128)} %get-tuple-element.8), channel_id=1, replica_groups=mesh['px'=8,'py'=4] {'px','py'}, use_global_device_ids=true, to_apply=%region_11.12 | all-reduce | flops 1 | bytes 8 | tf_op jit(solution)/shard_map/psum | solution.py:142
  1405.5 30.3 %all_to_all.335 = f32[4,1,131072]{2,1,0:T(1,128)} all-to-all(f32[4,1,131072]{2,1,0:T(1,128)} %reshape.119), channel_id=1, replica_groups=mesh['px'=8,'py'=4] {'py'}, dimensions={0} | all-to-all | bytes 4194304 | tf_op jit(solution)/shard_map/all_to_all | solution.py:65
  1435.8 8.9 reduce.12
  1481.0 54.2 %all_to_all.336 = f32[8,1,65536]{2,1,0:T(1,128)} all-to-all(f32[8,1,65536]{2,1,0:T(1,128)} %reshape.121), channel_id=1, replica_groups=mesh['px'=8,'py'=4] {'px'}, dimensions={0} | all-to-all | bytes 4194304 | tf_op jit(solution)/shard_map/all_to_all | solution.py:68
  1535.3 8.4 reduce.13
  1582.8 52.0 %all_to_all.337 = f32[8,1,65536]{2,1,0:T(1,128)} all-to-all(f32[8,1,65536]{2,1,0:T(1,128)} %reshape.123), channel_id=1, replica_groups=mesh['px'=8,'py'=4] {'px'}, dimensions={0} | all-to-all | bytes 4194304 | tf_op jit(solution)/shard_map/all_to_all | solution.py:79
  1634.7 8.4 reduce.14
  1674.3 30.1 %all_to_all.338 = f32[4,1,131072]{2,1,0:T(1,128)} all-to-all(f32[4,1,131072]{2,1,0:T(1,128)} %reshape.125), channel_id=1, replica_groups=mesh['px'=8,'py'=4] {'py'}, dimensions={0} | all-to-all | bytes 4194304 | tf_op jit(solution)/shard_map/all_to_all | solution.py:82
  1704.4 8.9 reduce.15
  1731.2 7.7 multiply_reduce_fusion
  1738.9 38.8 %psum.62 = f32[]{:T(128)} all-reduce(f32[]{:T(128)} %get-tuple-element.74), channel_id=1, replica_groups=mesh['px'=8,'py'=4] {'px','py'}, use_global_device_ids=true, to_apply=%region_13.14 | all-reduce | flops 1 | bytes 8 | tf_op jit(solution)/shard_map/psum | solution.py:135
  1798.9 40.3 %psum.63 = f32[]{:T(128)} all-reduce(f32[]{:T(128)} %fusion.6), channel_id=1, replica_groups=mesh['px'=8,'py'=4] {'px','py'}, use_global_device_ids=true, to_apply=%region_15.16 | all-reduce | flops 1 | bytes 8 | tf_op jit(solution)/shard_map/psum | solution.py:142
  1853.8 23.8 %all-to-all-done.17 = f32[32,64,256]{2,1,0:T(8,128)} async-done(((f32[32,64,256]{2,1,0:T(8,128)}), f32[32,64,256]{2,1,0:T(8,128)}, u32[]{:S(2)}, u32[]{:S(2)}) %all-to-all-start.17) | async-done | bytes 2097184 | tf_op jit(solution)/shard_map/all_to_all | solution.py:150
  (259 shorter events, 695.1 us)
Async XLA Ops:
  9.9 4.6 copy-start
  9.9 31.4 %all-to-all-start = ((f32[8,256,256]{2,0,1:T(8,128)}), f32[8,256,256]{2,0,1:T(8,128)}, u32[]{:S(2)}, u32[]{:S(2)}) async-start(f32[8,256,256]{2,0,1:T(8,128)} %get-tuple-element.19), calls=%async_computation | async-start | bytes 4194304 | tf_op jit(solution)/shard_map/all_to_all | solution.py:95
  14.5 10.2 collective-permute-start.2
  17.5 7.4 collective-permute-start
  26.4 27.9 %collective-permute-start.6 = (f32[34,1,256]{2,1,0:T(1,128)S(1)}, f32[34,1,256]{2,1,0:T(1,128)S(1)}, u32[]{:S(2)}, u32[]{:S(2)}) collective-permute-start(f32[34,1,256]{2,1,0:T(1,128)S(1)} %get-tuple-element.28), channel_id=1, source_target_pairs={{0,1},{1,2},{2,3},{3,0},{4,5},{5,6},{6,7},{7,4},{8,9},{9,10},{10,1... | collective-permute-start | bytes 104456 | tf_op jit(solution)/shard_map/ppermute | solution.py:32
  26.6 27.7 %collective-permute-start.4 = (f32[34,1,256]{2,1,0:T(1,128)S(1)}, f32[34,1,256]{2,1,0:T(1,128)S(1)}, u32[]{:S(2)}, u32[]{:S(2)}) collective-permute-start(f32[34,1,256]{2,1,0:T(1,128)S(1)} %get-tuple-element.29), channel_id=1, source_target_pairs={{1,0},{2,1},{3,2},{0,3},{5,4},{6,5},{7,6},{4,7},{9,8},{10,9},{11,1... | collective-permute-start | bytes 104456 | tf_op jit(solution)/shard_map/ppermute | solution.py:34
  43.5 11.9 copy-start.3
  43.6 8.2 collective-permute-start.3
  45.9 5.9 collective-permute-start.1
  51.8 2.5 collective-permute-start.5
  51.9 3.6 collective-permute-start.7
  162.7 53.6 %all-to-all-start.2 = ((f32[8,1,65536]{2,1,0:T(1,128)}), f32[8,1,65536]{2,1,0:T(1,128)}, u32[]{:S(2)}, u32[]{:S(2)}) async-start(f32[8,1,65536]{2,1,0:T(1,128)} %reshape.97), calls=%async_computation.2 | async-start | bytes 4194304 | tf_op jit(solution)/shard_map/all_to_all | solution.py:68
  418.4 7.5 collective-permute-start.9
  419.9 6.1 collective-permute-start.8
  423.2 6.3 copy-start.17
  423.2 6.3 copy-start.23
  426.0 3.6 copy-start.13
  426.0 1.9 collective-permute-start.10
  426.1 3.4 copy-start.5
  426.1 3.4 collective-permute-start.11
  873.8 11.6 copy-start.1
  873.8 7.1 collective-permute-start.13
  876.1 5.0 collective-permute-start.12
  878.6 6.8 copy-start.18
  881.1 4.3 copy-start.14
  881.1 1.7 collective-permute-start.14
  881.2 4.1 copy-start.6
  881.2 4.1 copy-start.10
  881.2 4.1 collective-permute-start.15
  1328.3 11.6 copy-start.2
  1328.3 7.1 collective-permute-start.17
  1330.7 5.0 collective-permute-start.16
  1333.1 6.8 copy-start.19
  1335.6 4.3 copy-start.15
  1335.7 1.7 collective-permute-start.18
  1335.8 4.2 copy-start.7
  1335.8 4.2 copy-start.11
  1335.8 4.1 collective-permute-start.19
  1781.6 7.1 collective-permute-start.21
  1784.0 5.0 collective-permute-start.20
  1786.4 6.8 copy-start.20
  1788.9 4.2 copy-start.16
  1789.0 1.7 collective-permute-start.22
  1789.1 4.1 copy-start.8
  1789.1 4.1 copy-start.12
  1789.1 4.1 collective-permute-start.23
  1847.3 4.6 copy-start.24
  1847.3 30.3 %all-to-all-start.17 = ((f32[32,64,256]{2,1,0:T(8,128)}), f32[32,64,256]{2,1,0:T(8,128)}, u32[]{:S(2)}, u32[]{:S(2)}) async-start(f32[32,64,256]{2,1,0:T(8,128)} %multiply_add_fusion.1), calls=%async_computation.17 | async-start | bytes 4194304 | tf_op jit(solution)/shard_map/all_to_all | solution.py:150
  (5 other events, 8.8 us)
where the time goes:
time: 1890 us; the launch traced here: 1880 us
  blocking collectives  889 us (47%)
  local copies, waits for them, and re-layouts  485 us (26%)
  other arithmetic  225 us (12%)
  matrix products  118 us (6%)
  waiting for transfers between devices  102 us (5%)
  starting transfers between devices  50.2 us (3%)
    all_to_all x4, blocking collectives, precondition_cas(): lax.all_to_all(spectrum, 'px', split_axis=0, concat_axis=1, tiled=True)  209 us
    unnamed x87, local copies, waits for them, and re-layouts  194 us
    all_to_all x3, blocking collectives, precondition_cas(): lax.all_to_all(spectrum, 'px', split_axis=1, concat_axis=0, tiled=True)  163 us
    psum x4, blocking collectives, product_sum(): return lax.psum(jnp.sum(residual * precond), ('px', 'py'))  155 us
    all_to_all x4, blocking collectives, precondition_cas(): lax.all_to_all(spectrum, 'py', split_axis=2, concat_axis=1, tiled=True)  121 us
    psum x3, blocking collectives, local(): alpha = product_now / lax.psum(jnp.sum(direction * image), ('px', 'py'))  121 us
    all_to_all x4, blocking collectives, precondition_cas(): lax.all_to_all(spectrum, 'py', split_axis=1, concat_axis=2, tiled=True)  120 us
    unnamed x16, matrix products  71.8 us
  transfers between devices with their start and end apart: 27, of which 17 were waited for; matrix products, arithmetic and copies ran while one was open for 1% of the time, Pallas kernels for 0%

commit v1 on v0

v1 whole, which is shorter than its diff:
```python
import math

import jax
import jax.numpy as jnp
import numpy as np
from jax import lax
from jax.sharding import PartitionSpec as P

ITERS = 4

mass_rate = 0.01
excite_gain = 8.0
threshold = 0.15
base_rate = 0.002
rate_slope = 0.2
rate_shift = 0.3
time_step = 0.1
AXES = ("px", "py")


def cas_table(length):
    steps = np.arange(length)
    angle = 2.0 * math.pi / length * (steps[:, None] * steps[None, :] % length)
    return np.cos(angle) + np.sin(angle)


def wave_term(length):
    return 2.0 - 2.0 * np.cos(2.0 * math.pi / length * np.arange(length))


def mode_tables(length_y, length_z):
    shift = mass_rate + wave_term(length_y)[:, None] + wave_term(length_z)[None, :]
    root = np.sqrt(shift * (4.0 + shift))
    rho = 2.0 / (2.0 + shift + root)
    scale = 1.0 / (root * length_y * length_z)
    return rho, scale


def local(potential, recovery, stimulus, conductivity):
    devices = lax.axis_size("px") * lax.axis_size("py")
    me = lax.axis_index(AXES)
    rows, length_y, length_z = potential.shape
    length_x = rows * devices
    forth = [(i, (i + 1) % devices) for i in range(devices)]
    back = [((i + 1) % devices, i) for i in range(devices)]
    drive = (
        excite_gain * potential * (potential - threshold) * (1.0 - potential) - potential * recovery
    )
    v_star = potential + time_step * (drive + stimulus)
    rate = base_rate + rate_slope * recovery / (potential + rate_shift)
    recovery_next = recovery + time_step * rate * (
        -recovery - excite_gain * potential * (potential - threshold - 1.0)
    )
    cond = lax.all_to_all(conductivity, "py", split_axis=0, concat_axis=1, tiled=True)

    def above(field):
        return lax.ppermute(field[:1], AXES, back)

    def below(field):
        return lax.ppermute(field[-1:], AXES, forth)

    cond_x = jnp.concatenate([below(cond), cond, above(cond)], 0)
    face_x = 0.5 * (cond_x[1:] + cond_x[:-1])
    face_y = 0.5 * (cond + jnp.roll(cond, -1, 1))
    face_z = 0.5 * (cond + jnp.roll(cond, -1, 2))

    def faces(field):
        padded = jnp.concatenate([below(field), field, above(field)], 0)
        flow_x = face_x * (padded[:-1] - padded[1:])
        flow_y = face_y * (field - jnp.roll(field, -1, 1))
        flow_z = face_z * (field - jnp.roll(field, -1, 2))
        return (
            (flow_x[1:] - flow_x[:-1])
            + (flow_y - jnp.roll(flow_y, 1, 1))
            + (flow_z - jnp.roll(flow_z, 1, 2))
        )

    rho64, scale64 = mode_tables(length_y, length_z)
    rho = jnp.asarray(rho64, jnp.float32)
    scale = jnp.asarray(scale64, jnp.float32)
    cas_y = jnp.asarray(cas_table(length_y), jnp.float32)
    cas_z = jnp.asarray(cas_table(length_z), jnp.float32)
    step_log = jnp.asarray(rows * np.log(rho64), jnp.float32)
    closing = jnp.asarray(1.0 / (1.0 - rho64**length_x), jnp.float32)
    part = length_y // devices
    step_log = lax.dynamic_slice_in_dim(step_log, me * part, part, 0)
    closing = lax.dynamic_slice_in_dim(closing, me * part, part, 0)
    order = np.arange(devices)
    gap = jnp.asarray((order[:, None] - 1 - order[None, :]) % devices, jnp.float32)

    def both(field):
        field = jnp.einsum("xyz,zk->xyk", field, cas_z, precision=lax.Precision.HIGH)
        return jnp.einsum("xyk,yq->xqk", field, cas_y, precision=lax.Precision.HIGH)

    def apply_inverse(residual):
        spectrum = both(residual)
        head = spectrum[rows - 1]
        tail = spectrum[0]
        for i in range(1, rows):
            head = head + rho**i * spectrum[rows - 1 - i]
            tail = tail + rho**i * spectrum[i]
        ends = jnp.stack([head, tail])[None]
        ends = lax.all_to_all(ends, AXES, split_axis=2, concat_axis=0, tiled=True)
        power = jnp.exp(gap[:, :, None, None] * step_log) * closing
        left = jnp.sum(power * ends[None, :, 0], 1)
        right = jnp.sum(jnp.swapaxes(power, 0, 1) * ends[None, :, 1], 1)
        carry = jnp.stack([left, right], 1)
        carry = lax.all_to_all(carry, AXES, split_axis=0, concat_axis=2, tiled=True)
        forward, backward = [None] * rows, [None] * rows
        value = carry[0, 0]
        for i in range(rows):
            value = spectrum[i] + rho * value
            forward[i] = value
        value = carry[0, 1]
        for i in reversed(range(rows)):
            backward[i] = rho * value
            value = spectrum[i] + backward[i]
        return both(jnp.stack([scale * (f + b) for f, b in zip(forward, backward)]))

    field = v_star
    residual = -faces(v_star)
    direction = image = gamma = alpha = None
    for step in range(ITERS):
        precond = apply_inverse(residual)
        applied = mass_rate * precond + faces(precond)
        sums = jnp.stack([jnp.sum(residual * precond), jnp.sum(applied * precond)])
        sums = jnp.sum(lax.all_gather(jnp.broadcast_to(sums[:, None], (2, 128)), AXES), 0)
        gamma_next, delta = sums[0, 0], sums[1, 0]
        if step == 0:
            alpha = gamma_next / delta
            direction, image = precond, applied
        else:
            beta = gamma_next / gamma
            alpha = gamma_next / (delta - beta * gamma_next / alpha)
            direction = precond + beta * direction
            image = applied + beta * image
        gamma = gamma_next
        field = field + alpha * direction
        residual = residual - alpha * image
    return (field, recovery_next)


def solution(mesh):
    in_specs = (
        P(AXES, None, None),
        P(AXES, None, None),
        P(AXES, None, None),
        P("px", "py", None),
    )
    out_specs = (P(AXES, None, None), P(AXES, None, None))
    return jax.shard_map(local, mesh=mesh, in_specs=in_specs, out_specs=out_specs, check_vma=False)
```

time: 1890 us -> 571 us (0.30)
  blocking collectives: 889 us -> 256 us
  local copies, waits for them, and re-layouts: 485 us -> 76.2 us
  other arithmetic: 225 us -> 87.5 us
  matrix products: 118 us -> 16.7 us
  waiting for transfers between devices: 102 us -> 59.5 us
    all_to_all x15 -> x5, blocking collectives: 613 us -> 103 us  [the longest x3 66.7 us: apply_inverse(): ends = lax.all_to_all(ends, AXES, split_axis=2, concat_axis=0, tiled=True)]
    psum x7 -> x0, blocking collectives: 276 us -> none  [the longest x4 155 us: product_sum(): return lax.psum(jnp.sum(residual * precond), ('px', 'py'))]
    all_to_all x35 -> x10, local copies, waits for them, and re-layouts: 186 us -> 7.41 us  [the longest x2 5.05 us: local(): lax.all_to_all(conductivity, 'py', split_axis=0, concat_axis=1, tiled=True)]
    unnamed x87 -> x171, local copies, waits for them, and re-layouts: 194 us -> 36.1 us
    unnamed x0 -> x4, blocking collectives: none -> 152 us
    all_to_all x16 -> x0, other arithmetic: 139 us -> none  [the longest x4 35.8 us: precondition_cas(): lax.all_to_all(spectrum, 'py', split_axis=1, concat_axis=2, tiled=True)]
    unnamed x16 -> x0, matrix products: 71.8 us -> none
    mul x8 -> x4, local copies, waits for them, and re-layouts: 45 us -> 0.15 us  [apply_inverse(): right = jnp.sum(jnp.swapaxes(power, 0, 1) * ends[None, :, 1], 1)]
  transfers between devices with their start and end apart: 27 -> 16, of which waited for: 17 -> 8; matrix products, arithmetic and copies ran while one was open for 1% -> 8% of each run, Pallas kernels for 0% -> 0%
where the time goes in v1:
time: 571 us; the launch traced here: 560 us
  blocking collectives  256 us (45%)
  other arithmetic  87.5 us (15%)
  local copies, waits for them, and re-layouts  76.2 us (13%)
  waiting for transfers between devices  59.5 us (10%)
  starting transfers between devices  49.1 us (9%)
  matrix products  16.7 us (3%)
  between operations  15.7 us (3%)
    unnamed x4, blocking collectives  152 us
    all_to_all x3, blocking collectives, apply_inverse(): ends = lax.all_to_all(ends, AXES, split_axis=2, concat_axis=0, tiled=True)  66.7 us
    all_to_all x2, blocking collectives, apply_inverse(): carry = lax.all_to_all(carry, AXES, split_axis=0, concat_axis=2, tiled=True)  36.8 us
    unnamed x171, local copies, waits for them, and re-layouts  36.1 us
    ppermute x6, starting transfers between devices, above(): return lax.ppermute(field[:1], AXES, back)  33.5 us
    all_to_all x2, waiting for transfers between devices, apply_inverse(): carry = lax.all_to_all(carry, AXES, split_axis=0, concat_axis=2, tiled=True)  28.3 us
    unnamed x32, other arithmetic  16.7 us
    reduce_sum x4, other arithmetic, apply_inverse(): left = jnp.sum(power * ends[None, :, 0], 1)  16.3 us
  transfers between devices with their start and end apart: 16, of which 8 were waited for; matrix products, arithmetic and copies ran while one was open for 8% of the time, Pallas kernels for 0%

profile of v1, /device:TPU:0, one launch (start us, length us, event | category | flops | bytes accessed | tf_op | source)
XLA Modules:
  0.0 560.5 jit_solution(8653421226274850138)
XLA Ops:
  0.6 4.6 all-to-all-start
  7.1 3.0 copy.192
  11.9 4.5 multiply_add_fusion
  17.7 6.6 %collective-permute-start.3 = (f32[1,256,256]{1,2,0:T(8,128)S(1)}, f32[1,256,256]{1,2,0:T(8,128)}, u32[]{:S(2)}, u32[]{:S(2)}) collective-permute-start(f32[1,256,256]{1,2,0:T(8,128)S(1)} %get-tuple-element.85), channel_id=1, source_target_pairs={{1,0},{2,1},{3,2},{4,3},{5,4},{6,5},{7,6},{8,7},{9,8},{10,9},{11,1... | collective-permute-start | bytes 786440 | tf_op jit(solution)/shard_map/ppermute | solution.py:57
  28.9 5.6 all-to-all-done
  34.5 3.1 copy.193
  45.6 5.4 collective-permute-start
  51.0 7.2 %fusion.26 = (f32[8,256,256]{1,2,0:T(8,128)S(1)}, f32[8,256,256]{1,2,0:T(8,128)}, f32[8,256,256]{1,2,0:T(8,128)S(1)}, f32[8,256,256]{1,2,0:T(8,128)}) fusion(f32[8,256,256]{1,2,0:T(8,128)} %copy-done.8, f32[8,256,1]{1,2,0:T(1,128)S(1)} %slice.635, f32[8,256,255]{1,2,0:T(8,128)} %slice.634, f32[8,256,256]{1,2,0:T(8,128)S(1)} %copy.195, ...), kind=kLoop, calls=%fused_computation.52 | loop fusion | flops 6291456 | bytes 20971520 | tf_op jit(solution)/shard_map/mul | solution.py:71
  67.9 3.0 all-to-all-start.1
  71.6 14.9 %all-to-all-done.1 = f32[1,2,256,256]{3,1,0,2:T(2,128)S(1)} async-done(((f32[1,2,256,256]{3,1,0,2:T(2,128)}), f32[1,2,256,256]{3,1,0,2:T(2,128)S(1)}, u32[]{:S(2)}, u32[]{:S(2)}) %all-to-all-start.1) | async-done | bytes 524320 | tf_op jit(solution)/shard_map/all_to_all | solution.py:103
  86.6 4.1 multiply_reduce_fusion.7
  91.6 3.7 all-to-all-start.2
  95.3 15.6 %all-to-all-done.2 = f32[32,2,8,256]{3,2,1,0:T(8,128)} async-done(((f32[32,2,8,256]{3,2,1,0:T(8,128)}), f32[32,2,8,256]{3,2,1,0:T(8,128)}, u32[]{:S(2)}, u32[]{:S(2)}) %all-to-all-start.2) | async-done | bytes 524320 | tf_op jit(solution)/shard_map/all_to_all | solution.py:108
  116.3 2.0 bitcast_dynamic-update-slice_fusion.31
  123.5 5.3 collective-permute-start.5
  130.2 2.7 collective-permute-done.4
  133.4 3.7 multiply_reduce_fusion.14
  138.4 38.0 %all-reduce = f32[64]{0:T(128)S(1)} all-reduce(f32[64]{0:T(128)S(1)} %maximum_dynamic-update-slice_fusion), channel_id=6, replica_groups=mesh['px'=8,'py'=4] {'px','py'}, use_global_device_ids=true, to_apply=%add | all-reduce | flops 64 | bytes 512
  178.6 2.5 multiply_subtract_fusion.2
  188.1 22.5 %all_to_all.162 = f32[1,2,256,256]{3,1,0,2:T(2,128)S(1)} all-to-all(f32[1,2,256,256]{3,1,0,2:T(2,128)} %copy.217), channel_id=1, replica_groups=mesh['px'=8,'py'=4] {'px','py'}, dimensions={2} | all-to-all | bytes 1048576 | tf_op jit(solution)/shard_map/all_to_all | solution.py:103
  210.7 4.1 multiply_reduce_fusion.5
  214.9 18.4 %all_to_all.163 = f32[32,2,8,256]{3,2,1,0:T(8,128)S(1)} all-to-all(f32[32,2,8,256]{3,2,1,0:T(8,128)S(1)} %copy.219), channel_id=1, replica_groups=mesh['px'=8,'py'=4] {'px','py'}, dimensions={0} | all-to-all | bytes 1048576 | tf_op jit(solution)/shard_map/all_to_all | solution.py:108
  237.7 2.0 bitcast_dynamic-update-slice_fusion.23
  244.9 5.3 collective-permute-start.7
  251.6 2.7 collective-permute-done.6
  254.8 3.6 multiply_reduce_fusion.12
  259.7 38.1 %all-reduce.1 = f32[64]{0:T(128)S(1)} all-reduce(f32[64]{0:T(128)S(1)} %maximum_dynamic-update-slice_fusion.1), channel_id=7, replica_groups=mesh['px'=8,'py'=4] {'px','py'}, use_global_device_ids=true, to_apply=%add.1 | all-reduce | flops 64 | bytes 512
  303.2 3.3 multiply_subtract_fusion.1
  313.6 22.1 %all_to_all.164 = f32[1,2,256,256]{3,1,0,2:T(2,128)S(1)} all-to-all(f32[1,2,256,256]{3,1,0,2:T(2,128)} %copy.228), channel_id=1, replica_groups=mesh['px'=8,'py'=4] {'px','py'}, dimensions={2} | all-to-all | bytes 1048576 | tf_op jit(solution)/shard_map/all_to_all | solution.py:103
  335.8 4.1 multiply_reduce_fusion.3
  340.0 18.4 %all_to_all.165 = f32[32,2,8,256]{3,2,1,0:T(8,128)S(1)} all-to-all(f32[32,2,8,256]{3,2,1,0:T(8,128)S(1)} %copy.230), channel_id=1, replica_groups=mesh['px'=8,'py'=4] {'px','py'}, dimensions={0} | all-to-all | bytes 1048576 | tf_op jit(solution)/shard_map/all_to_all | solution.py:108
  370.0 5.5 collective-permute-start.9
  376.9 2.6 collective-permute-done.8
  379.8 3.6 multiply_reduce_fusion.10
  384.8 38.2 %all-reduce.2 = f32[64]{0:T(128)S(1)} all-reduce(f32[64]{0:T(128)S(1)} %maximum_dynamic-update-slice_fusion.2), channel_id=8, replica_groups=mesh['px'=8,'py'=4] {'px','py'}, use_global_device_ids=true, to_apply=%add.2 | all-reduce | flops 64 | bytes 512
  427.4 4.0 multiply_subtract_fusion
  436.5 2.0 copy.239
  438.5 22.1 %all_to_all.166 = f32[1,2,256,256]{3,1,0,2:T(2,128)S(1)} all-to-all(f32[1,2,256,256]{3,1,0,2:T(2,128)} %copy.239), channel_id=1, replica_groups=mesh['px'=8,'py'=4] {'px','py'}, dimensions={2} | all-to-all | bytes 1048576 | tf_op jit(solution)/shard_map/all_to_all | solution.py:103
  460.7 4.1 multiply_reduce_fusion.1
  465.7 3.6 all-to-all-start.8
  469.3 2.9 copy.254
  472.2 12.7 %all-to-all-done.8 = f32[32,2,8,256]{3,2,1,0:T(8,128)} async-done(((f32[32,2,8,256]{3,2,1,0:T(8,128)}), f32[32,2,8,256]{3,2,1,0:T(8,128)}, u32[]{:S(2)}, u32[]{:S(2)}) %all-to-all-start.8) | async-done | bytes 524320 | tf_op jit(solution)/shard_map/all_to_all | solution.py:108
  495.0 5.3 collective-permute-start.11
  501.7 2.7 collective-permute-done.10
  504.8 2.6 multiply_reduce_fusion.8
  508.8 38.0 %all-reduce.3 = f32[64]{0:T(128)S(1)} all-reduce(f32[64]{0:T(128)S(1)} %maximum_dynamic-update-slice_fusion.3), channel_id=9, replica_groups=mesh['px'=8,'py'=4] {'px','py'}, use_global_device_ids=true, to_apply=%add.3 | all-reduce | flops 64 | bytes 512
  551.3 5.8 %multiply_add_fusion.1 = f32[8,256,256]{1,2,0:T(8,128)} fusion(f32[8,256,256]{1,2,0:T(8,128)} %copy-done.7, f32[8,256,256]{1,2,0:T(8,128)} %copy-done.6, f32[8,256,256]{1,2,0:T(8,128)} %copy-done.5, f32[8,256,256]{1,2,0:T(8,128)S(1)} %copy-done.4, f32[8,256,256]{1,2,0:T(8,128)} %copy-done.8, f32[]{:T(128)S(6)} %div.40, f32[]{:T(128)S(6)} %div.42, ...), kind=kLoop, calls=%fused_computation.79 | loop fusion | flops 7340032 | bytes 12582940 | tf_op jit(solution)/shard_map/add | solution.py:138
  557.1 2.9 copy.253
  (341 shorter events, 106.1 us)
Async XLA Ops:
  0.6 4.6 copy-start.73
  0.6 33.8 %all-to-all-start = ((f32[32,64,256]{2,1,0:T(8,128)}), f32[32,64,256]{2,1,0:T(8,128)}, u32[]{:S(2)}, u32[]{:S(2)}) async-start(f32[32,64,256]{2,1,0:T(8,128)} %param.14), calls=%async_computation | async-start | bytes 4194304 | tf_op jit(solution)/shard_map/all_to_all | solution.py:54
  7.1 3.0 copy-start.74
  16.4 10.6 %copy-start.8 = (f32[8,256,256]{1,2,0:T(8,128)}, f32[8,256,256]{1,2,0:T(8,128)S(1)}, u32[]{:S(2)}) copy-start(f32[8,256,256]{1,2,0:T(8,128)S(1)} %get-tuple-element.64) | copy-start | bytes 6291460
  17.2 41.3 %collective-permute-start.2 = (f32[1,256,256]{1,2,0:T(8,128)}, f32[1,256,256]{1,2,0:T(8,128)}, u32[]{:S(2)}, u32[]{:S(2)}) collective-permute-start(f32[1,256,256]{1,2,0:T(8,128)} %get-tuple-element.86), channel_id=1, source_target_pairs={{0,1},{1,2},{2,3},{3,4},{4,5},{5,6},{6,7},{7,8},{8,9},{9,10},{10,1... | collective-permute-start | bytes 786440 | tf_op jit(solution)/shard_map/ppermute | solution.py:60
  17.7 40.8 %collective-permute-start.3 = (f32[1,256,256]{1,2,0:T(8,128)S(1)}, f32[1,256,256]{1,2,0:T(8,128)}, u32[]{:S(2)}, u32[]{:S(2)}) collective-permute-start(f32[1,256,256]{1,2,0:T(8,128)S(1)} %get-tuple-element.85), channel_id=1, source_target_pairs={{1,0},{2,1},{3,2},{4,3},{5,4},{6,5},{7,6},{8,7},{9,8},{10,9},{11,1... | collective-permute-start | bytes 786440 | tf_op jit(solution)/shard_map/ppermute | solution.py:57
  45.4 13.1 %collective-permute-start.1 = (f32[1,256,256]{1,2,0:T(8,128)S(1)}, f32[1,256,256]{1,2,0:T(8,128)S(1)}, u32[]{:S(2)}, u32[]{:S(2)}) collective-permute-start(f32[1,256,256]{1,2,0:T(8,128)S(1)} %copy.196), channel_id=1, source_target_pairs={{0,1},{1,2},{2,3},{3,4},{4,5},{5,6},{6,7},{7,8},{8,9},{9,10},{10,1... | collective-permute-start | bytes 786440 | tf_op jit(solution)/shard_map/ppermute | solution.py:60
  45.6 12.9 %collective-permute-start = (f32[1,256,256]{1,2,0:T(8,128)S(1)}, f32[1,256,256]{1,2,0:T(8,128)S(1)}, u32[]{:S(2)}, u32[]{:S(2)}) collective-permute-start(f32[1,256,256]{1,2,0:T(8,128)S(1)} %copy.194), channel_id=1, source_target_pairs={{1,0},{2,1},{3,2},{4,3},{5,4},{6,5},{7,6},{8,7},{9,8},{10,9},{11,1... | collective-permute-start | bytes 786440 | tf_op jit(solution)/shard_map/ppermute | solution.py:57
  66.9 19.7 %copy-start.75 = (f32[32,32]{1,0:T(8,128)S(1)}, f32[32,32]{1,0:T(8,128)}, u32[]{:S(2)}) copy-start(f32[32,32]{1,0:T(8,128)} %constant.59.clone) | copy-start | bytes 12292
  66.9 19.7 %copy-start.76 = (f32[32,32]{1,0:T(8,128)S(1)}, f32[32,32]{1,0:T(8,128)}, u32[]{:S(2)}) copy-start(f32[32,32]{1,0:T(8,128)} %constant.69) | copy-start | bytes 12292
  67.9 18.6 %all-to-all-start.1 = ((f32[1,2,256,256]{3,1,0,2:T(2,128)}), f32[1,2,256,256]{3,1,0,2:T(2,128)S(1)}, u32[]{:S(2)}, u32[]{:S(2)}) async-start(f32[1,2,256,256]{3,1,0,2:T(2,128)} %copy.206), calls=%async_computation.1 | async-start | bytes 1048576 | tf_op jit(solution)/shard_map/all_to_all | solution.py:103
  91.6 24.7 %copy-start.1 = (f32[256,256]{0,1:T(8,128)S(1)}, f32[256,256]{0,1:T(8,128)}, u32[]{:S(2)}) copy-start(f32[256,256]{0,1:T(8,128)} %constant.55.clone) | copy-start | bytes 786436
  91.6 24.7 %copy-start.2 = (f32[1,1,256,256]{2,3,1,0:T(8,128)S(1)}, f32[1,1,256,256]{2,3,1,0:T(8,128)}, u32[]{:S(2)}) copy-start(f32[1,1,256,256]{2,3,1,0:T(8,128)} %constant.70) | copy-start | bytes 786436
  91.6 19.3 %all-to-all-start.2 = ((f32[32,2,8,256]{3,2,1,0:T(8,128)}), f32[32,2,8,256]{3,2,1,0:T(8,128)}, u32[]{:S(2)}, u32[]{:S(2)}) async-start(f32[32,2,8,256]{3,2,1,0:T(8,128)} %copy.208), calls=%async_computation.2 | async-start | bytes 1048576 | tf_op jit(solution)/shard_map/all_to_all | solution.py:108
  122.4 10.9 %copy-start.3 = (f32[8,256,256]{1,2,0:T(8,128)}, f32[8,256,256]{1,2,0:T(8,128)S(1)}, u32[]{:S(2)}) copy-start(f32[8,256,256]{1,2,0:T(8,128)S(1)} %convolution_bitcast_fusion.6) | copy-start | bytes 6291460
  123.1 5.7 %copy-start.19 = (f32[8,256,256]{1,2,0:T(8,128)S(1)}, f32[8,256,256]{1,2,0:T(8,128)}, u32[]{:S(2)}) copy-start(f32[8,256,256]{1,2,0:T(8,128)} %get-tuple-element.60) | copy-start | bytes 6291460
  123.1 5.7 %copy-start.23 = (f32[8,256,256]{1,2,0:T(8,128)S(1)}, f32[8,256,256]{1,2,0:T(8,128)}, u32[]{:S(2)}) copy-start(f32[8,256,256]{1,2,0:T(8,128)} %get-tuple-element.66) | copy-start | bytes 6291460
  123.4 9.5 %collective-permute-start.4 = (f32[1,256,256]{1,2,0:T(8,128)S(1)}, f32[1,256,256]{1,2,0:T(8,128)S(1)}, u32[]{:S(2)}, u32[]{:S(2)}) collective-permute-start(f32[1,256,256]{1,2,0:T(8,128)S(1)} %get-tuple-element.80), channel_id=1, source_target_pairs={{0,1},{1,2},{2,3},{3,4},{4,5},{5,6},{6,7},{7,8},{8,9},{9,10},{10,1... | collective-permute-start | bytes 786440 | tf_op jit(solution)/shard_map/ppermute | solution.py:60
  123.5 9.5 %collective-permute-start.5 = (f32[1,256,256]{1,2,0:T(8,128)S(1)}, f32[1,256,256]{1,2,0:T(8,128)S(1)}, u32[]{:S(2)}, u32[]{:S(2)}) collective-permute-start(f32[1,256,256]{1,2,0:T(8,128)S(1)} %get-tuple-element.79), channel_id=1, source_target_pairs={{1,0},{2,1},{3,2},{4,3},{5,4},{6,5},{7,6},{8,7},{9,8},{10,9},{11,1... | collective-permute-start | bytes 786440 | tf_op jit(solution)/shard_map/ppermute | solution.py:57
  129.8 3.1 copy-start.60
  129.9 3.1 copy-start.65
  130.2 3.1 copy-start.28
  243.8 10.9 %copy-start.5 = (f32[8,256,256]{1,2,0:T(8,128)}, f32[8,256,256]{1,2,0:T(8,128)S(1)}, u32[]{:S(2)}) copy-start(f32[8,256,256]{1,2,0:T(8,128)S(1)} %convolution_bitcast_fusion.4) | copy-start | bytes 6291460
  244.5 5.7 %copy-start.20 = (f32[8,256,256]{1,2,0:T(8,128)S(1)}, f32[8,256,256]{1,2,0:T(8,128)}, u32[]{:S(2)}) copy-start(f32[8,256,256]{1,2,0:T(8,128)} %get-tuple-element.60) | copy-start | bytes 6291460
  244.6 5.7 %copy-start.24 = (f32[8,256,256]{1,2,0:T(8,128)S(1)}, f32[8,256,256]{1,2,0:T(8,128)}, u32[]{:S(2)}) copy-start(f32[8,256,256]{1,2,0:T(8,128)} %get-tuple-element.66) | copy-start | bytes 6291460
  244.8 9.5 %collective-permute-start.6 = (f32[1,256,256]{1,2,0:T(8,128)S(1)}, f32[1,256,256]{1,2,0:T(8,128)S(1)}, u32[]{:S(2)}, u32[]{:S(2)}) collective-permute-start(f32[1,256,256]{1,2,0:T(8,128)S(1)} %get-tuple-element.76), channel_id=1, source_target_pairs={{0,1},{1,2},{2,3},{3,4},{4,5},{5,6},{6,7},{7,8},{8,9},{9,10},{10,1... | collective-permute-start | bytes 786440 | tf_op jit(solution)/shard_map/ppermute | solution.py:60
  244.9 9.5 %collective-permute-start.7 = (f32[1,256,256]{1,2,0:T(8,128)S(1)}, f32[1,256,256]{1,2,0:T(8,128)S(1)}, u32[]{:S(2)}, u32[]{:S(2)}) collective-permute-start(f32[1,256,256]{1,2,0:T(8,128)S(1)} %get-tuple-element.75), channel_id=1, source_target_pairs={{1,0},{2,1},{3,2},{4,3},{5,4},{6,5},{7,6},{8,7},{9,8},{10,9},{11,1... | collective-permute-start | bytes 786440 | tf_op jit(solution)/shard_map/ppermute | solution.py:57
  251.2 3.1 copy-start.61
  251.3 3.1 copy-start.66
  251.6 3.1 copy-start.30
  368.9 10.9 %copy-start.6 = (f32[8,256,256]{1,2,0:T(8,128)}, f32[8,256,256]{1,2,0:T(8,128)S(1)}, u32[]{:S(2)}) copy-start(f32[8,256,256]{1,2,0:T(8,128)S(1)} %convolution_bitcast_fusion.2) | copy-start | bytes 6291460
  369.6 5.9 %copy-start.21 = (f32[8,256,256]{1,2,0:T(8,128)S(1)}, f32[8,256,256]{1,2,0:T(8,128)}, u32[]{:S(2)}) copy-start(f32[8,256,256]{1,2,0:T(8,128)} %get-tuple-element.60) | copy-start | bytes 6291460
  369.6 5.9 %copy-start.25 = (f32[8,256,256]{1,2,0:T(8,128)S(1)}, f32[8,256,256]{1,2,0:T(8,128)}, u32[]{:S(2)}) copy-start(f32[8,256,256]{1,2,0:T(8,128)} %get-tuple-element.66) | copy-start | bytes 6291460
  369.9 9.5 %collective-permute-start.8 = (f32[1,256,256]{1,2,0:T(8,128)S(1)}, f32[1,256,256]{1,2,0:T(8,128)S(1)}, u32[]{:S(2)}, u32[]{:S(2)}) collective-permute-start(f32[1,256,256]{1,2,0:T(8,128)S(1)} %get-tuple-element.72), channel_id=1, source_target_pairs={{0,1},{1,2},{2,3},{3,4},{4,5},{5,6},{6,7},{7,8},{8,9},{9,10},{10,1... | collective-permute-start | bytes 786440 | tf_op jit(solution)/shard_map/ppermute | solution.py:60
  370.0 9.5 %collective-permute-start.9 = (f32[1,256,256]{1,2,0:T(8,128)S(1)}, f32[1,256,256]{1,2,0:T(8,128)S(1)}, u32[]{:S(2)}, u32[]{:S(2)}) collective-permute-start(f32[1,256,256]{1,2,0:T(8,128)S(1)} %get-tuple-element.71), channel_id=1, source_target_pairs={{1,0},{2,1},{3,2},{4,3},{5,4},{6,5},{7,6},{8,7},{9,8},{10,9},{11,1... | collective-permute-start | bytes 786440 | tf_op jit(solution)/shard_map/ppermute | solution.py:57
  376.5 2.9 copy-start.62
  376.5 2.9 copy-start.67
  376.9 2.9 copy-start.32
  465.7 19.2 %all-to-all-start.8 = ((f32[32,2,8,256]{3,2,1,0:T(8,128)}), f32[32,2,8,256]{3,2,1,0:T(8,128)}, u32[]{:S(2)}, u32[]{:S(2)}) async-start(f32[32,2,8,256]{3,2,1,0:T(8,128)} %copy.241), calls=%async_computation.8 | async-start | bytes 1048576 | tf_op jit(solution)/shard_map/all_to_all | solution.py:108
  493.9 10.9 %copy-start.7 = (f32[8,256,256]{1,2,0:T(8,128)}, f32[8,256,256]{1,2,0:T(8,128)S(1)}, u32[]{:S(2)}) copy-start(f32[8,256,256]{1,2,0:T(8,128)S(1)} %convolution_bitcast_fusion) | copy-start | bytes 6291460
  494.6 5.7 %copy-start.22 = (f32[8,256,256]{1,2,0:T(8,128)S(1)}, f32[8,256,256]{1,2,0:T(8,128)}, u32[]{:S(2)}) copy-start(f32[8,256,256]{1,2,0:T(8,128)} %get-tuple-element.60) | copy-start | bytes 6291460
  494.6 5.7 %copy-start.26 = (f32[8,256,256]{1,2,0:T(8,128)S(1)}, f32[8,256,256]{1,2,0:T(8,128)}, u32[]{:S(2)}) copy-start(f32[8,256,256]{1,2,0:T(8,128)} %get-tuple-element.66) | copy-start | bytes 6291460
  494.9 9.5 %collective-permute-start.10 = (f32[1,256,256]{1,2,0:T(8,128)S(1)}, f32[1,256,256]{1,2,0:T(8,128)S(1)}, u32[]{:S(2)}, u32[]{:S(2)}) collective-permute-start(f32[1,256,256]{1,2,0:T(8,128)S(1)} %get-tuple-element.68), channel_id=1, source_target_pairs={{0,1},{1,2},{2,3},{3,4},{4,5},{5,6},{6,7},{7,8},{8,9},{9,10},{10,1... | collective-permute-start | bytes 786440 | tf_op jit(solution)/shard_map/ppermute | solution.py:60
  495.0 9.5 %collective-permute-start.11 = (f32[1,256,256]{1,2,0:T(8,128)S(1)}, f32[1,256,256]{1,2,0:T(8,128)S(1)}, u32[]{:S(2)}, u32[]{:S(2)}) collective-permute-start(f32[1,256,256]{1,2,0:T(8,128)S(1)} %get-tuple-element.67), channel_id=1, source_target_pairs={{1,0},{2,1},{3,2},{4,3},{5,4},{6,5},{7,6},{8,7},{9,8},{10,9},{11,1... | collective-permute-start | bytes 786440 | tf_op jit(solution)/shard_map/ppermute | solution.py:57
  501.3 3.1 copy-start.63
  501.3 3.1 copy-start.68
  501.7 3.1 copy-start.34
  504.8 46.5 %copy-start.4 = (f32[8,256,256]{1,2,0:T(8,128)S(1)}, f32[8,256,256]{1,2,0:T(8,128)}, u32[]{:S(2)}) copy-start(f32[8,256,256]{1,2,0:T(8,128)} %copy-done.3) | copy-start | bytes 6291460
  (45 other events, 64.9 us)

commit v2 on v1

--- a/solution.py
+++ b/solution.py
@@ -4,6 +4,8 @@
 import jax.numpy as jnp
 import numpy as np
 from jax import lax
+from jax.experimental import pallas as pl
+from jax.experimental.pallas import tpu as pltpu
 from jax.sharding import PartitionSpec as P
 
 ITERS = 4
@@ -140,6 +142,314 @@
     return (field, recovery_next)
 
 
+def split(table):
+    high = table.astype(jnp.bfloat16)
+    low = (table - high.astype(np.float64)).astype(jnp.bfloat16)
+    return jnp.asarray(high), jnp.asarray(low)
+
+
+def parts_of(block):
+    high = block.astype(jnp.bfloat16)
+    return high, (block - high.astype(jnp.float32)).astype(jnp.bfloat16)
+
+
+def product(left, right):
+    def dot(a, b):
+        return jnp.dot(a, b, preferred_element_type=jnp.float32)
+
+    return dot(left[0], right[1]) + dot(left[1], right[0]) + dot(left[0], right[0])
+
+
+def kernel(
+    v_ref, cond_in, yh_ref, yl_ref, zh_ref, zl_ref, rho_ref, scale_ref, sigma_ref, close_ref,
+    u_ref,
+    cond, face_x, face_y, face_z, res, dire, imag, z_ref, w_ref, spec, back_ref, power,
+    ends, recv, sol, carry, mine, gath,
+    c_send, c_recv, h_send, h_recv, e_send, e_recv, s_send, s_recv, g_send, g_recv,
+):
+    count_y = lax.axis_size("py")
+    devices = lax.axis_size("px") * count_y
+    my_y = lax.axis_index("py")
+    me = lax.axis_index("px") * count_y + my_y
+    rows, length_y, length_z = v_ref.shape
+    part = length_y // devices
+    wide_y = cond_in.shape[1]
+    mesh_type = pl.DeviceIdType.MESH
+
+    def device(index):
+        return (index // count_y, index % count_y)
+
+    def strip(index):
+        return pl.ds(pl.multiple_of(index * part, part), part)
+
+    def halo(buffer, base):
+        left = (me + devices - 1) % devices
+        right = (me + 1) % devices
+        return (
+            pltpu.make_async_remote_copy(
+                buffer.at[1], buffer.at[rows + 1], h_send.at[base], h_recv.at[base],
+                device_id=device(left), device_id_type=mesh_type,
+            ),
+            pltpu.make_async_remote_copy(
+                buffer.at[rows], buffer.at[0], h_send.at[base + 1], h_recv.at[base + 1],
+                device_id=device(right), device_id_type=mesh_type,
+            ),
+        )
+
+    def start_all(make, count):
+        def begin(k, _):
+            make(k).start()
+            return 0
+
+        lax.fori_loop(1, count, begin, 0)
+
+    def wait_all(make, count):
+        def finish(k, _):
+            make(k).wait()
+            return 0
+
+        lax.fori_loop(1, count, finish, 0)
+
+    def cond_copy(k):
+        other = (my_y + k) % count_y
+        return pltpu.make_async_remote_copy(
+            cond_in.at[pl.ds(other * rows, rows)],
+            cond.at[pl.ds(1, rows), pl.ds(pl.multiple_of(my_y * wide_y, 8), wide_y), :],
+            c_send.at[k], c_recv.at[k],
+            device_id=(lax.axis_index("px"), other), device_id_type=mesh_type,
+        )
+
+    def ends_copy(k):
+        other = (me + k) % devices
+        return pltpu.make_async_remote_copy(
+            ends.at[:, strip(other), :], recv.at[me], e_send.at[k], e_recv.at[k],
+            device_id=device(other), device_id_type=mesh_type,
+        )
+
+    def carry_copy(k):
+        other = (me + k) % devices
+        return pltpu.make_async_remote_copy(
+            sol.at[other], carry.at[:, strip(me), :], s_send.at[k], s_recv.at[k],
+            device_id=device(other), device_id_type=mesh_type,
+        )
+
+    def gath_copy(k):
+        other = (me + k) % devices
+        return pltpu.make_async_remote_copy(
+            mine, gath.at[me], g_send.at[k], g_recv.at[k],
+            device_id=device(other), device_id_type=mesh_type,
+        )
+
+    def stencil(k, _):
+        i = (k + 1) % rows
+        here = z_ref[i + 1]
+        total = face_x[i + 1] * (here - z_ref[i + 2]) - face_x[i] * (z_ref[i] - here)
+        flow = face_y[i] * (here - pltpu.roll(here, length_y - 1, 0))
+        total = total + (flow - pltpu.roll(flow, 1, 0))
+        flow = face_z[i] * (here - pltpu.roll(here, length_z - 1, 1))
+        w_ref[i] = total + (flow - pltpu.roll(flow, 1, 1))
+        return 0
+
+    start_all(cond_copy, count_y)
+    for i in range(rows):
+        z_ref[i + 1] = v_ref[i]
+        u_ref[i] = v_ref[i]
+    field_halo = halo(z_ref, 0)
+    for copy in field_halo:
+        copy.start()
+    cond[pl.ds(1, rows), pl.ds(pl.multiple_of(my_y * wide_y, 8), wide_y), :] = cond_in[
+        pl.ds(my_y * rows, rows)
+    ]
+    wait_all(cond_copy, count_y)
+    cond_halo = halo(cond, 2)
+    for copy in cond_halo:
+        copy.start()
+
+    def faces(i, _):
+        here = cond[i + 1]
+        face_y[i] = 0.5 * (here + pltpu.roll(here, length_y - 1, 0))
+        face_z[i] = 0.5 * (here + pltpu.roll(here, length_z - 1, 1))
+        return 0
+
+    lax.fori_loop(0, rows, faces, 0)
+    for copy in cond_halo + field_halo:
+        copy.wait()
+
+    def faces_along(i, _):
+        face_x[i] = 0.5 * (cond[i] + cond[i + 1])
+        return 0
+
+    lax.fori_loop(0, rows + 1, faces_along, 0)
+    lax.fori_loop(0, rows, stencil, 0)
+
+    def first(i, _):
+        res[i] = -w_ref[i]
+        dire[i] = jnp.zeros((length_y, length_z), jnp.float32)
+        imag[i] = jnp.zeros((length_y, length_z), jnp.float32)
+        return 0
+
+    lax.fori_loop(0, rows, first, 0)
+
+    def iteration(step, scalars):
+        gamma, alpha = scalars
+        ends[...] = jnp.zeros_like(ends)
+        power[...] = jnp.ones_like(power)
+
+        def ahead(i, _):
+            block = product(parts_of(res[i]), (zh_ref[...], zl_ref[...]))
+            block = product((yh_ref[...], yl_ref[...]), parts_of(block))
+            spec[i] = block
+            rho = rho_ref[...]
+            ends[0] = block + rho * ends[0]
+            ends[1] = ends[1] + power[...] * block
+            power[...] = power[...] * rho
+            return 0
+
+        lax.fori_loop(0, rows, ahead, 0)
+        start_all(ends_copy, devices)
+        recv[me] = ends[:, strip(me), :]
+        wait_all(ends_copy, devices)
+
+        sigma = sigma_ref[strip(me), :]
+        close = close_ref[strip(me), :]
+        zero = jnp.zeros_like(sigma)
+
+        def sums(b, pair):
+            return (
+                recv[b, 0] + sigma * pair[0],
+                recv[devices - 1 - b, 1] + sigma * pair[1],
+            )
+
+        pair = lax.fori_loop(0, devices, sums, (zero, zero), unroll=4)
+
+        def place(b, pair):
+            c = devices - 1 - b
+            sol[b, 0] = pair[0]
+            sol[c, 1] = pair[1]
+            return sums(b, pair)
+
+        lax.fori_loop(0, devices, place, (pair[0] * close, pair[1] * close), unroll=4)
+        start_all(carry_copy, devices)
+        carry[:, strip(me), :] = sol[me]
+        wait_all(carry_copy, devices)
+
+        def behind(j, _):
+            i = rows - 1 - j
+            value = rho_ref[...] * carry[1]
+            back_ref[i] = value
+            carry[1] = spec[i] + value
+            return 0
+
+        lax.fori_loop(0, rows, behind, 0)
+
+        def inverse(i, _):
+            value = spec[i] + rho_ref[...] * carry[0]
+            carry[0] = value
+            value = scale_ref[...] * (value + back_ref[i])
+            value = product((yh_ref[...], yl_ref[...]), parts_of(value))
+            z_ref[i + 1] = product(parts_of(value), (zh_ref[...], zl_ref[...]))
+            return 0
+
+        lax.fori_loop(0, rows, inverse, 0)
+        copies = halo(z_ref, 0)
+        for copy in copies:
+            copy.start()
+        lax.fori_loop(0, rows - 2, stencil, 0)
+        for copy in copies:
+            copy.wait()
+        lax.fori_loop(rows - 2, rows, stencil, 0)
+
+        mine[...] = jnp.zeros_like(mine)
+
+        def fold(value):
+            value = jnp.sum(value.reshape(length_y // 8, 8, length_z), 0)
+            return sum(value[:, c : c + 128] for c in range(0, length_z, 128))
+
+        def dots(i, _):
+            z = z_ref[i + 1]
+            applied = mass_rate * z + w_ref[i]
+            w_ref[i] = applied
+            mine[0] = mine[0] + fold(z * res[i])
+            mine[1] = mine[1] + fold(z * applied)
+            return 0
+
+        lax.fori_loop(0, rows, dots, 0)
+        start_all(gath_copy, devices)
+        gath[me] = mine[...]
+        wait_all(gath_copy, devices)
+        total = jnp.sum(gath[...], 0)
+        gamma_next = jnp.sum(total[0], keepdims=True)
+        delta = jnp.sum(total[1], keepdims=True)
+        beta = jnp.where(step == 0, 0.0, gamma_next / gamma)
+        alpha_next = gamma_next / (delta - beta * gamma_next / alpha)
+
+        def update(i, _):
+            direction = z_ref[i + 1] + beta * dire[i]
+            image = w_ref[i] + beta * imag[i]
+            dire[i] = direction
+            imag[i] = image
+            u_ref[i] = u_ref[i] + alpha_next * direction
+            res[i] = res[i] - alpha_next * image
+            return 0
+
+        lax.fori_loop(0, rows, update, 0)
+        return gamma_next, alpha_next
+
+    one = jnp.ones((1, 1), jnp.float32)
+    lax.fori_loop(0, ITERS, iteration, (one, one))
+
+
+def fused(potential, recovery, stimulus, conductivity):
+    devices = lax.axis_size("px") * lax.axis_size("py")
+    rows, length_y, length_z = potential.shape
+    part = length_y // devices
+    if part % 8 or length_z % 128 or conductivity.shape[1] % 8:
+        return local(potential, recovery, stimulus, conductivity)
+    drive = (
+        excite_gain * potential * (potential - threshold) * (1.0 - potential) - potential * recovery
+    )
+    v_star = potential + time_step * (drive + stimulus)
+    rate = base_rate + rate_slope * recovery / (potential + rate_shift)
+    recovery_next = recovery + time_step * rate * (
+        -recovery - excite_gain * potential * (potential - threshold - 1.0)
+    )
+    rho, scale = mode_tables(length_y, length_z)
+    tables = split(cas_table(length_y)) + split(cas_table(length_z))
+    tables += tuple(
+        jnp.asarray(table, jnp.float32)
+        for table in (rho, scale, rho**rows, 1.0 / (1.0 - rho ** (rows * devices)))
+    )
+    plane = (length_y, length_z)
+    whole = (rows,) + plane
+
+    def vmem(shape):
+        return pltpu.VMEM(shape, jnp.float32)
+
+    dma = pltpu.SemaphoreType.DMA
+    padded = (rows + 2,) + plane
+    slots = (devices, 2, part, length_z)
+    field = pl.pallas_call(
+        kernel,
+        out_shape=jax.ShapeDtypeStruct(whole, jnp.float32),
+        in_specs=[pl.BlockSpec(memory_space=pltpu.VMEM)] * 10,
+        out_specs=pl.BlockSpec(memory_space=pltpu.VMEM),
+        scratch_shapes=[
+            vmem(padded), vmem((rows + 1,) + plane), vmem(whole), vmem(whole),
+            vmem(whole), vmem(whole), vmem(whole), vmem(padded), vmem(whole),
+            vmem(whole), vmem(whole), vmem(plane),
+            vmem((2,) + plane), vmem(slots), vmem(slots), vmem((2,) + plane),
+            vmem((2, 8, 128)), vmem((devices, 2, 8, 128)),
+            dma((devices,)), dma((devices,)), dma((4,)), dma((4,)),
+            dma((devices,)), dma((devices,)), dma((devices,)), dma((devices,)),
+            dma((devices,)), dma((devices,)),
+        ],
+        compiler_params=pltpu.CompilerParams(
+            has_side_effects=True, vmem_limit_bytes=56 * 1024 * 1024
+        ),
+    )(v_star, conductivity, *tables)
+    return (field, recovery_next)
+
+
 def solution(mesh):
     in_specs = (
         P(AXES, None, None),
@@ -148,4 +458,4 @@
         P("px", "py", None),
     )
     out_specs = (P(AXES, None, None), P(AXES, None, None))
-    return jax.shard_map(local, mesh=mesh, in_specs=in_specs, out_specs=out_specs, check_vma=False)
+    return jax.shard_map(fused, mesh=mesh, in_specs=in_specs, out_specs=out_specs, check_vma=False)

time: 571 us -> 277 us (0.49); the launches traced: 560 us -> 277 us
  Pallas kernels: 0 us -> 268 us
  blocking collectives: 256 us -> 0 us
  other arithmetic: 87.5 us -> 4.88 us
  local copies, waits for them, and re-layouts: 76.2 us -> 3.8 us
  waiting for transfers between devices: 59.5 us -> 0 us
  starting transfers between devices: 49.1 us -> 0 us
  matrix products: 16.7 us -> 0 us
  between operations: 15.7 us -> 0.64 us
    pallas_call x0 -> x1, Pallas kernels: none -> 268 us  [fused(): pl.pallas_call(kernel, out_shape=jax.ShapeDtypeStruct(whole, jnp.float32)...]
    unnamed x4 -> x0, blocking collectives: 152 us -> none
    all_to_all x5 -> x0, blocking collectives: 103 us -> none  [the longest x3 66.7 us: apply_inverse(): ends = lax.all_to_all(ends, AXES, split_axis=2, concat_axis=0, tiled=True)]
    all_to_all x4 -> x0, waiting for transfers between devices: 48.7 us -> none  [the longest x2 28.3 us: apply_inverse(): carry = lax.all_to_all(carry, AXES, split_axis=0, concat_axis=2, tiled=True)]
    ppermute x12 -> x0, starting transfers between devices: 34.3 us -> none  [the longest x6 33.5 us: above(): return lax.ppermute(field[:1], AXES, back)]
    unnamed x171 -> x1, local copies, waits for them, and re-layouts: 36.1 us -> 3.05 us
    reduce_sum x12 -> x0, other arithmetic: 30.1 us -> none  [the longest x4 16.3 us: apply_inverse(): left = jnp.sum(power * ends[None, :, 0], 1)]
    slice x50 -> x0, local copies, waits for them, and re-layouts: 22.3 us -> none  [the longest x10 5.66 us: faces(): flow_y = face_y * (field - jnp.roll(field, -1, 1))]
  transfers between devices with their start and end apart: 16 -> 0, of which waited for: 8 -> 0; matrix products, arithmetic and copies ran while one was open for 8% -> 0% of each run, Pallas kernels for 0% -> 0%
where the time goes in v2:
time: 277 us
  Pallas kernels  268 us (97%)
  other arithmetic  4.88 us (2%)
  local copies, waits for them, and re-layouts  3.8 us (1%)
    pallas_call x1, Pallas kernels, fused(): pl.pallas_call(kernel, out_shape=jax.ShapeDtypeStruct(whole, jnp.float32)...  268 us

profile of v2, /device:TPU:0, one launch (start us, length us, event | category | flops | bytes accessed | tf_op | source)
XLA Modules:
  0.0 277.0 jit_solution(11014324677663106630)
XLA Ops:
  0.6 4.9 %multiply_add_fusion = (f32[8,256,256]{2,1,0:T(8,128)}, f32[8,256,256]{2,1,0:T(8,128)}) fusion(f32[8,256,256]{2,1,0:T(8,128)} %param.13, f32[8,256,256]{2,1,0:T(8,128)} %param.12, f32[8,256,256]{2,1,0:T(8,128)} %param.14), kind=kLoop, calls=%fused_computation | loop fusion | flops 11010048 | bytes 10485760 | tf_op jit(solution)/shard_map/add | solution.py:413
  5.5 0.8 jit_solution_.3.close_ref
  6.3 267.6 %shard_map.131 = f32[8,256,256]{2,1,0:T(8,128)} custom-call(f32[8,256,256]{2,1,0:T(8,128)} %get-tuple-element.3.v_ref, f32[32,64,256]{2,1,0:T(8,128)} %cond_in.1, bf16[256,256]{1,0:T(8,128)(2,1)} %constant.30.clone.yh_ref.zh_ref, bf16[256,256]{1,0:T(8,128)(2,1)} %constant.31.clone.yl_ref.zl_ref, bf16[256,256]{1,0:T(8,128)(2,1)} %constant.30.clone.yh_ref.zh_ref, ...), custom_call_target="tpu_custom_call" | custom-call | tf_op jit(solution)/shard_map/pallas_call | solution.py:431
  273.9 3.0 %copy.15 = f32[8,256,256]{2,1,0:T(8,128)} copy(f32[8,256,256]{2,1,0:T(8,128)} %shard_map.131) | data formatting | bytes 4194304
